TPU v7x, 256 devices: a whole 4x4x8 slice. The times are simulated.
256 devices in a mesh: seq: 64 (over z, y, core), head: 4 (over x).
Axes of the slice: x: 4, y: 4, z: 8, core: 2. Of those that a mesh axis runs over, the one named last changes fastest.
Arguments:
- query_rows: bfloat16 [131072, 4096], P(('seq', 'head')), may hold values from -200 to 200
- key_rows: bfloat16 [131072, 512], P(('seq', 'head')), may hold values from -18 to 18
- value_rows: bfloat16 [131072, 512], P(('seq', 'head')), may hold values from -6 to 6
- random_table: int32 [1024, 4, 3], replicated, may hold values from 0 to 1023, as said below
- global_blocks: int32 [2], replicated, may hold values from 0 to 1023
Outputs:
- attended: bfloat16 [131072, 4096], P(('seq', 'head'))
Inputs may be any that keep to these rules, and one draw needn't show every extreme that they name: `random_table`: for each of the 4 head groups and each aligned run of 16 query blocks (those of one index of seq), with the owner of block j being j // 16: at most 2 of the run's 3 * 16 entries name blocks of one owner, and they name at most 1 distinct blocks of one owner; both bounds are reached.
All inputs are finite; a program needn't handle non-finite values.
Results may differ from a plain program's by a relative error of at most 0.0029.
Values may be sent and summed in bfloat16 or wider, within the bound.
A program may use at most 128 MiB of HBM per device.

v0:
```python
import math
import jax
import jax.numpy as jnp
from jax import lax
from jax.sharding import PartitionSpec as P

BLOCK = 128
HEAD_DIM = 128
GLOBALS = 2
RANDOM = 3


def padded_2(cells, sides, width):
    for axis, dim in sides:
        count = lax.axis_size(axis)
        ends = count - 1
        head = lax.slice_in_dim(cells, 0, width, axis=dim)
        tail = lax.slice_in_dim(cells, cells.shape[dim] - width, cells.shape[dim], axis=dim)
        cells = jnp.concatenate(
            [
                lax.ppermute(tail, axis, [(i, (i + 1) % count) for i in range(ends)]),
                cells,
                lax.ppermute(head, axis, [((i + 1) % count, i) for i in range(ends)]),
            ],
            axis=dim,
        )
    return cells


def picked(shard, axis, root):
    return lax.dynamic_index_in_dim(lax.all_gather(shard, axis), root, 0, keepdims=False)


def attend_group(query_group, context, usable, score_scale):
    key_part = context[..., :HEAD_DIM]
    values = context[..., HEAD_DIM:]
    scores = (
        jnp.einsum("ptgd,psd->pgts", query_group, key_part, preferred_element_type=jnp.float32)
        * score_scale
    )
    scores = jnp.where(usable[:, None, None, :], scores, -1e30)
    row_max = jnp.max(scores, axis=-1, keepdims=True)
    weights = jnp.exp(scores - row_max)
    row_total = jnp.sum(weights, axis=-1)
    rounded = weights.astype(jnp.bfloat16)
    mixed = jnp.einsum("pgts,psd->ptgd", rounded, values, preferred_element_type=jnp.float32)
    mixed = mixed / jnp.transpose(row_total, (0, 2, 1))[..., None]
    return mixed.astype(jnp.bfloat16)


def on_device(query_rows, key_rows, value_rows, random_table, global_blocks):
    queries, key_part, values = (
        lax.all_to_all(query_rows, "head", split_axis=1, concat_axis=0, tiled=True),
        lax.all_to_all(key_rows, "head", split_axis=1, concat_axis=0, tiled=True),
        lax.all_to_all(value_rows, "head", split_axis=1, concat_axis=0, tiled=True),
    )
    local_rows = queries.shape[0]
    block_count = local_rows // BLOCK
    grouping = queries.shape[1] // HEAD_DIM
    seq_count = lax.axis_size("seq")
    seq_index = lax.axis_index("seq")
    head_index = lax.axis_index("head")
    paired = jnp.concatenate([key_part, values], axis=1)
    local_blocks = paired.reshape(block_count, BLOCK, 2 * HEAD_DIM)
    padded = padded_2(paired, (("seq", 0),), BLOCK)
    global_parts = []
    for global_index in range(GLOBALS):
        named_block = global_blocks[global_index]
        piece = lax.dynamic_index_in_dim(local_blocks, named_block % block_count, 0, keepdims=False)
        global_parts.append(picked(piece, "seq", named_block // block_count))
    shared = jnp.stack(global_parts)
    table_head = lax.dynamic_index_in_dim(random_table, head_index, 1, keepdims=False)
    all_refs = table_head.reshape(seq_count, block_count * RANDOM)
    my_refs = lax.dynamic_index_in_dim(all_refs, seq_index, 0, keepdims=False)
    owner_all = all_refs // block_count
    local_all = all_refs % block_count
    my_owner = my_refs // block_count
    my_local = my_refs % block_count
    entry_bound = 2 * max(1, (RANDOM * block_count + 2 * seq_count - 1) // (2 * seq_count))
    capacity = entry_bound // 2
    block_range = jnp.arange(block_count, dtype=jnp.int32)
    hits = (owner_all[:, :, None] == seq_index) & (local_all[:, :, None] == block_range)
    requested = jnp.any(hits, axis=1)
    distinct_rank = jnp.cumsum(requested.astype(jnp.int32), axis=1) - 1
    selected = requested[:, :, None] & (
        distinct_rank[:, :, None] == jnp.arange(capacity, dtype=jnp.int32)
    )
    sources = jnp.sum(jnp.where(selected, block_range[None, :, None], 0), axis=1)
    filled = jnp.any(selected, axis=1)
    outgoing = jnp.take(local_blocks, sources, axis=0)
    outgoing = jnp.where(filled[:, :, None, None], outgoing, jnp.zeros_like(outgoing))
    received = lax.all_to_all(outgoing, "seq", split_axis=0, concat_axis=0, tiled=True)
    my_requested = jnp.any(
        my_refs[:, None] == jnp.arange(seq_count * block_count, dtype=jnp.int32)[None, :], axis=0
    )
    owner_lines = my_requested.reshape(seq_count, block_count)[my_owner]
    my_slot = jnp.sum(
        (owner_lines & (block_range[None, :] < my_local[:, None])).astype(jnp.int32), axis=1
    )
    fetched = received[my_owner, my_slot].reshape(block_count, RANDOM * BLOCK, 2 * HEAD_DIM)
    previous = padded[:local_rows].reshape(block_count, BLOCK, 2 * HEAD_DIM)
    upcoming = padded[2 * BLOCK :].reshape(block_count, BLOCK, 2 * HEAD_DIM)
    shared_all = jnp.broadcast_to(
        shared.reshape(1, GLOBALS * BLOCK, 2 * HEAD_DIM),
        (block_count, GLOBALS * BLOCK, 2 * HEAD_DIM),
    )
    context = jnp.concatenate([previous, local_blocks, upcoming, shared_all, fetched], axis=1)
    global_ids = seq_index * block_count + jnp.arange(block_count, dtype=jnp.int32)
    block_flags = jnp.concatenate(
        [
            (global_ids > 0)[:, None],
            (global_ids >= 0)[:, None],
            (global_ids < seq_count * block_count - 1)[:, None],
            jnp.ones((block_count, GLOBALS + RANDOM), dtype=bool),
        ],
        axis=1,
    )
    usable = jnp.repeat(block_flags, BLOCK, axis=1)
    per_step = max((size_try for size_try in (1, 2, 3, 4) if block_count % size_try == 0))
    step_count = block_count // per_step
    score_scale = 1.0 / math.sqrt(HEAD_DIM)
    query_steps = queries.reshape(step_count, per_step, BLOCK, grouping, HEAD_DIM)
    context_steps = context.reshape(step_count, per_step, context.shape[1], 2 * HEAD_DIM)
    usable_steps = usable.reshape(step_count, per_step, usable.shape[1])

    def one_step(inputs):
        return attend_group(inputs[0], inputs[1], inputs[2], score_scale)

    mixed = lax.map(one_step, (query_steps, context_steps, usable_steps))
    output_rows = mixed.reshape(local_rows, grouping * HEAD_DIM)
    return lax.all_to_all(output_rows, "head", split_axis=0, concat_axis=1, tiled=True)


def solution(mesh):
    placed = (
        P(("seq", "head"), None),
        P(("seq", "head"), None),
        P(("seq", "head"), None),
        P(),
        P(),
    )
    return jax.shard_map(
        on_device, mesh=mesh, in_specs=placed, out_specs=P(("seq", "head"), None), check_vma=False
    )
```

profile of v0, /device:TPU:1, one launch (start us, length us, event | category | flops | bytes accessed | tf_op | source)
XLA Modules:
  0.0 373.1 jit_solution(15213330352972939691)
XLA Ops:
  8.5 4.8 %all-to-all-start = ((bf16[512,4,128]{2,0,1:T(8,128)(2,1)}), bf16[512,4,128]{2,0,1:T(8,128)(2,1)S(1)}, u32[]{:S(2)}, u32[]{:S(2)}) async-start(bf16[512,4,128]{2,0,1:T(8,128)(2,1)} %copy_bitcast_fusion.4), calls=%async_computation | async-start | bytes 1048576 | tf_op jit(solution)/shard_map/all_to_all | solution.py:54
  13.3 1.9 copy_bitcast_fusion.3
  15.2 5.5 %all-to-all-done = bf16[512,4,128]{2,0,1:T(8,128)(2,1)S(1)} async-done(((bf16[512,4,128]{2,0,1:T(8,128)(2,1)}), bf16[512,4,128]{2,0,1:T(8,128)(2,1)S(1)}, u32[]{:S(2)}, u32[]{:S(2)}) %all-to-all-start) | async-done | bytes 524320 | tf_op jit(solution)/shard_map/all_to_all | solution.py:54
  20.8 3.5 all-to-all-start.1
  28.8 2.3 all-to-all-done.1
  31.8 4.7 %copy.90 = bf16[64,4,8,1024]{3,2,0,1:T(8,128)(2,1)} copy(bf16[64,4,8,1024]{3,2,1,0:T(8,128)(2,1)} %bitcast.165) | data formatting | bytes 8388608 | tf_op jit(solution)/shard_map/all_to_all | solution.py:53
  36.6 4.9 %all-to-all-start.3 = ((bf16[512,4,1024]{2,0,1:T(8,128)(2,1)}), bf16[512,4,1024]{2,0,1:T(8,128)(2,1)}, u32[]{:S(2)}, u32[]{:S(2)}) async-start(bf16[512,4,1024]{2,0,1:T(8,128)(2,1)} %bitcast.159), calls=%async_computation.3 | async-start | bytes 8388608 | tf_op jit(solution)/shard_map/all_to_all | solution.py:53
  43.9 2.8 gather_fusion
  46.7 4.0 %fusion.16 = bf16[64,1,128,256]{3,2,1,0:T(8,128)(2,1)} fusion(bf16[64,128,256]{2,1,0:T(8,128)(2,1)} %gather_fusion, pred[64]{0:T(512)(128)(4,1)S(1)} %compare_and_fusion, pred[64]{0:T(512)(128)(4,1)S(1)} %get-tuple-element.70), kind=kLoop, calls=%fused_computation.27 | loop fusion | flops 4194304 | bytes 8388736 | tf_op jit(solution)/shard_map/jit(_where)/select_n | solution.py:91
  50.7 35.6 %all-to-all-done.3 = bf16[512,4,1024]{2,0,1:T(8,128)(2,1)} async-done(((bf16[512,4,1024]{2,0,1:T(8,128)(2,1)}), bf16[512,4,1024]{2,0,1:T(8,128)(2,1)}, u32[]{:S(2)}, u32[]{:S(2)}) %all-to-all-start.3) | async-done | bytes 4194336 | tf_op jit(solution)/shard_map/all_to_all | solution.py:53
  86.3 17.9 %all-to-all-start.2 = ((bf16[64,1,128,256]{3,2,1,0:T(8,128)(2,1)}), bf16[64,1,128,256]{3,2,1,0:T(8,128)(2,1)}, u32[]{:S(2)}, u32[]{:S(2)}) async-start(bf16[64,1,128,256]{3,2,1,0:T(8,128)(2,1)} %fusion.16), calls=%async_computation.2 | async-start | bytes 8388608 | tf_op jit(solution)/shard_map/all_to_all | solution.py:92
  105.5 3.5 collective-permute-start
  109.0 1.9 collective-permute-start.1
  112.5 2.1 collective-permute-done
  114.5 2.6 collective-permute-done.1
  117.3 1.1 constant_dynamic-update-slice_fusion.3
  118.4 1.1 maximum_dynamic-update-slice_fusion
  119.5 1.1 constant_dynamic-update-slice_fusion.2
  120.6 5.2 %copy.82 = bf16[256,8,8,128]{3,2,1,0:T(8,128)(2,1)} copy(bf16[256,8,8,128]{3,1,2,0:T(8,128)(2,1)} %bitcast.53) | data formatting | bytes 8388608
  126.6 88.3 %all-gather.3.cloned.1.call-done = bf16[64,128,256]{2,1,0:T(8,128)(2,1)} async-done(((bf16[1,128,256]{2,1,0:T(8,128)(2,1)}), bf16[64,128,256]{2,1,0:T(8,128)(2,1)}) %all-gather.3.cloned.1.call-update) | async-done | bytes 4194320 | tf_op jit(solution)/shard_map/all_gather | solution.py:31
  215.8 1.5 broadcast_dynamic-update-slice_fusion
  217.4 4.6 %gather_fusion.2 = bf16[48,128,256]{2,1,0:T(8,128)(2,1)} fusion(bf16[64,1,128,256]{3,2,1,0:T(8,128)(2,1)} %all-to-all-done.2, s32[48]{0:T(128)S(1)} %fusion.35), kind=kCustom, calls=%fused_computation.2 | custom fusion | bytes 6291840 | tf_op jit(solution)/shard_map/gather | solution.py:100
  222.0 3.8 %constant_dynamic-update-slice_fusion.1 = bf16[4,4,1024,256]{3,2,1,0:T(8,128)(2,1)} fusion(bf16[4,4,1024,256]{3,2,1,0:T(8,128)(2,1)} %broadcast_dynamic-update-slice_fusion, bf16[4,4,384,256]{3,2,1,0:T(8,128)(2,1)} %bitcast.162), kind=kLoop, calls=%fused_computation.66 | loop fusion | bytes 6291456 | tf_op jit(solution)/shard_map/concatenate | solution.py:107
  225.8 66.2 %while.10 = (s32[]{:T(128)}, bf16[4,4,128,8,128]{4,3,2,1,0:T(8,128)(2,1)}, bf16[4,4,1024,256]{3,2,1,0:T(8,128)(2,1)}, pred[4,4,1024]{2,1,0:T(4,128)(4,1)S(1)}, bf16[4,4,128,8,128]{4,3,2,1,0:T(8,128)(2,1)}, /*index=5*/s32[]{:T(128)}) while((s32[]{:T(128)}, bf16[4,4,128,8,128]{4,3,2,1,0:T(8,128)(2,1)}, bf16[4,4,1024,256]{3,2,1,0:T(8,128)(2,1)}, ...), condition=%wide.region_9.10_spmd, body=%wide.region_6.9_spmd.sunk | while | flops 2194661376 | bytes 65114704 | solution.py:129
  225.8 1.7 dynamic-slice_bitcast_fusion.5
  227.6 1.3 constant_dynamic-slice_fusion.6
  228.9 3.0 bitcast_reduce_fusion.2
  231.9 3.7 %fusion.48 = f32[4,8,128]{2,1,0:T(8,128)S(1)} fusion(f32[4,1024,128,8]{2,1,3,0:T(8,128)S(1)} %get-tuple-element.117, f32[4,8,128]{2,1,0:T(8,128)S(1)} %get-tuple-element.118, pred[4,1024]{1,0:T(4,128)(4,1)S(1)} %dynamic-slice_bitcast_fusion.4), kind=kLoop, calls=%fused_computation.7.clone.1 | loop fusion | flops 16773120 | bytes 16814080 | tf_op jit(solution)/shard_map/while/body/eval_jaxpr/reduce_sum | solution.py:44
  235.7 4.9 %fusion.49 = bf16[1,4,128,8,128]{2,4,3,1,0:T(8,128)(2,1)S(1)} fusion(f32[4,1024,128,8]{2,1,3,0:T(8,128)S(1)} %get-tuple-element.117, f32[4,8,128]{2,1,0:T(8,128)S(1)} %get-tuple-element.118, pred[4,1024]{1,0:T(4,128)(4,1)S(1)} %dynamic-slice_bitcast_fusion.4, bf16[4,1024,256]{2,1,0:T(8,128)(2,1)S(1)} %dynamic-slice_bitcast_fusion.5, ...), kind=kOutput, calls=%fused_computation.14.clone.1 | convolution fusion | flops 1091567616 | bytes 18911232 | tf_op jit(solution)/shard_map/while/body/eval_jaxpr/pgts,psd->ptgd/dot_general | solution.py:46
  242.4 1.7 dynamic-slice_bitcast_fusion.5
  244.1 1.3 constant_dynamic-slice_fusion.6
  245.4 3.0 bitcast_reduce_fusion.2
  248.5 3.7 %fusion.48 = f32[4,8,128]{2,1,0:T(8,128)S(1)} fusion(f32[4,1024,128,8]{2,1,3,0:T(8,128)S(1)} %get-tuple-element.117, f32[4,8,128]{2,1,0:T(8,128)S(1)} %get-tuple-element.118, pred[4,1024]{1,0:T(4,128)(4,1)S(1)} %dynamic-slice_bitcast_fusion.4), kind=kLoop, calls=%fused_computation.7.clone.1 | loop fusion | flops 16773120 | bytes 16814080 | tf_op jit(solution)/shard_map/while/body/eval_jaxpr/reduce_sum | solution.py:44
  252.2 4.9 %fusion.49 = bf16[1,4,128,8,128]{2,4,3,1,0:T(8,128)(2,1)S(1)} fusion(f32[4,1024,128,8]{2,1,3,0:T(8,128)S(1)} %get-tuple-element.117, f32[4,8,128]{2,1,0:T(8,128)S(1)} %get-tuple-element.118, pred[4,1024]{1,0:T(4,128)(4,1)S(1)} %dynamic-slice_bitcast_fusion.4, bf16[4,1024,256]{2,1,0:T(8,128)(2,1)S(1)} %dynamic-slice_bitcast_fusion.5, ...), kind=kOutput, calls=%fused_computation.14.clone.1 | convolution fusion | flops 1091567616 | bytes 18911232 | tf_op jit(solution)/shard_map/while/body/eval_jaxpr/pgts,psd->ptgd/dot_general | solution.py:46
  258.9 1.7 dynamic-slice_bitcast_fusion.5
  260.7 1.3 constant_dynamic-slice_fusion.6
  262.0 3.0 bitcast_reduce_fusion.2
  265.0 3.7 %fusion.48 = f32[4,8,128]{2,1,0:T(8,128)S(1)} fusion(f32[4,1024,128,8]{2,1,3,0:T(8,128)S(1)} %get-tuple-element.117, f32[4,8,128]{2,1,0:T(8,128)S(1)} %get-tuple-element.118, pred[4,1024]{1,0:T(4,128)(4,1)S(1)} %dynamic-slice_bitcast_fusion.4), kind=kLoop, calls=%fused_computation.7.clone.1 | loop fusion | flops 16773120 | bytes 16814080 | tf_op jit(solution)/shard_map/while/body/eval_jaxpr/reduce_sum | solution.py:44
  268.8 5.0 %fusion.49 = bf16[1,4,128,8,128]{2,4,3,1,0:T(8,128)(2,1)S(1)} fusion(f32[4,1024,128,8]{2,1,3,0:T(8,128)S(1)} %get-tuple-element.117, f32[4,8,128]{2,1,0:T(8,128)S(1)} %get-tuple-element.118, pred[4,1024]{1,0:T(4,128)(4,1)S(1)} %dynamic-slice_bitcast_fusion.4, bf16[4,1024,256]{2,1,0:T(8,128)(2,1)S(1)} %dynamic-slice_bitcast_fusion.5, ...), kind=kOutput, calls=%fused_computation.14.clone.1 | convolution fusion | flops 1091567616 | bytes 18911232 | tf_op jit(solution)/shard_map/while/body/eval_jaxpr/pgts,psd->ptgd/dot_general | solution.py:46
  275.5 1.7 dynamic-slice_bitcast_fusion.5
  277.2 1.3 constant_dynamic-slice_fusion.6
  278.5 3.0 bitcast_reduce_fusion.2
  281.6 3.7 %fusion.48 = f32[4,8,128]{2,1,0:T(8,128)S(1)} fusion(f32[4,1024,128,8]{2,1,3,0:T(8,128)S(1)} %get-tuple-element.117, f32[4,8,128]{2,1,0:T(8,128)S(1)} %get-tuple-element.118, pred[4,1024]{1,0:T(4,128)(4,1)S(1)} %dynamic-slice_bitcast_fusion.4), kind=kLoop, calls=%fused_computation.7.clone.1 | loop fusion | flops 16773120 | bytes 16814080 | tf_op jit(solution)/shard_map/while/body/eval_jaxpr/reduce_sum | solution.py:44
  285.3 5.0 %fusion.49 = bf16[1,4,128,8,128]{2,4,3,1,0:T(8,128)(2,1)S(1)} fusion(f32[4,1024,128,8]{2,1,3,0:T(8,128)S(1)} %get-tuple-element.117, f32[4,8,128]{2,1,0:T(8,128)S(1)} %get-tuple-element.118, pred[4,1024]{1,0:T(4,128)(4,1)S(1)} %dynamic-slice_bitcast_fusion.4, bf16[4,1024,256]{2,1,0:T(8,128)(2,1)S(1)} %dynamic-slice_bitcast_fusion.5, ...), kind=kOutput, calls=%fused_computation.14.clone.1 | convolution fusion | flops 1091567616 | bytes 18911232 | tf_op jit(solution)/shard_map/while/body/eval_jaxpr/pgts,psd->ptgd/dot_general | solution.py:46
  292.1 7.3 %all_to_all.69 = bf16[4,512,1024]{2,1,0:T(8,128)(2,1)} reshape(bf16[4,4,128,8,128]{4,3,2,1,0:T(8,128)(2,1)} %get-tuple-element.32) | data formatting | bytes 8388608 | tf_op jit(solution)/shard_map/all_to_all | solution.py:131
  299.4 54.3 %all_to_all.78 = bf16[4,512,1024]{2,1,0:T(8,128)(2,1)} all-to-all(bf16[4,512,1024]{2,1,0:T(8,128)(2,1)} %all_to_all.69), channel_id=1, replica_groups=mesh['seq'=64,'head'=4] {'head'}, dimensions={0} | all-to-all | bytes 8388608 | tf_op jit(solution)/shard_map/all_to_all | solution.py:131
  353.7 6.3 %copy.69 = bf16[512,4,1024]{0,2,1:T(8,128)(2,1)} copy(bf16[512,4,1024]{2,0,1:T(8,128)(2,1)} %bitcast.160) | data formatting | bytes 8388608 | tf_op jit(solution)/shard_map/all_to_all | solution.py:131
  359.9 6.4 %copy.70 = bf16[512,4096]{1,0:T(8,128)(2,1)} copy(bf16[512,4096]{0,1:T(8,128)(2,1)} %bitcast.161) | data formatting | bytes 8388608 | tf_op jit(solution)/shard_map/all_to_all | solution.py:131
  (65 shorter events, 15.9 us)
Async XLA Ops:
  6.5 1.0 copy-start
  6.5 17.8 %copy-start.2 = (s32[2]{0:T(128)S(1)}, s32[2]{0:T(128)}, u32[]{:S(2)}) copy-start(s32[2]{0:T(128)} %param.11) | copy-start | bytes 28
  8.5 12.3 %all-to-all-start = ((bf16[512,4,128]{2,0,1:T(8,128)(2,1)}), bf16[512,4,128]{2,0,1:T(8,128)(2,1)S(1)}, u32[]{:S(2)}, u32[]{:S(2)}) async-start(bf16[512,4,128]{2,0,1:T(8,128)(2,1)} %copy_bitcast_fusion.4), calls=%async_computation | async-start | bytes 1048576 | tf_op jit(solution)/shard_map/all_to_all | solution.py:54
  20.8 10.4 %all-to-all-start.1 = ((bf16[512,4,128]{2,0,1:T(8,128)(2,1)}), bf16[512,4,128]{2,0,1:T(8,128)(2,1)S(1)}, u32[]{:S(2)}, u32[]{:S(2)}) async-start(bf16[512,4,128]{2,0,1:T(8,128)(2,1)} %copy_bitcast_fusion.3), calls=%async_computation.1 | async-start | bytes 1048576 | tf_op jit(solution)/shard_map/all_to_all | solution.py:55
  24.2 101.6 %all-gather.5.cloned.1.call-start = ((), (), s32[]{:S(2)}) async-start(), calls=%async_computation.6 | async-start | bytes 4259840 | tf_op jit(solution)/shard_map/all_gather | solution.py:31
  36.6 49.8 %all-to-all-start.3 = ((bf16[512,4,1024]{2,0,1:T(8,128)(2,1)}), bf16[512,4,1024]{2,0,1:T(8,128)(2,1)}, u32[]{:S(2)}, u32[]{:S(2)}) async-start(bf16[512,4,1024]{2,0,1:T(8,128)(2,1)} %bitcast.159), calls=%async_computation.3 | async-start | bytes 8388608 | tf_op jit(solution)/shard_map/all_to_all | solution.py:53
  41.5 173.5 %all-gather.3.cloned.1.call-start = ((), (), s32[]{:S(2)}) async-start(), calls=%async_computation.5 | async-start | bytes 4259840 | tf_op jit(solution)/shard_map/all_gather | solution.py:31
  86.3 131.1 %all-to-all-start.2 = ((bf16[64,1,128,256]{3,2,1,0:T(8,128)(2,1)}), bf16[64,1,128,256]{3,2,1,0:T(8,128)(2,1)}, u32[]{:S(2)}, u32[]{:S(2)}) async-start(bf16[64,1,128,256]{3,2,1,0:T(8,128)(2,1)} %fusion.16), calls=%async_computation.2 | async-start | bytes 8388608 | tf_op jit(solution)/shard_map/all_to_all | solution.py:92
  105.5 9.0 %collective-permute-start = (bf16[128,256]{1,0:T(8,128)(2,1)S(1)}, bf16[128,256]{1,0:T(8,128)(2,1)S(1)}, u32[]{:S(2)}, u32[]{:S(2)}) collective-permute-start(bf16[128,256]{1,0:T(8,128)(2,1)S(1)} %get-tuple-element.79), channel_id=1, source_target_pairs={{0,4},{4,8},{8,12},{12,16},{16,20},{20,24},{24,28},{28,32},{32,36}... | collective-permute-start | bytes 196616 | tf_op jit(solution)/shard_map/ppermute | solution.py:21
  109.0 8.1 %collective-permute-start.1 = (bf16[128,256]{1,0:T(8,128)(2,1)S(1)}, bf16[128,256]{1,0:T(8,128)(2,1)S(1)}, u32[]{:S(2)}, u32[]{:S(2)}) collective-permute-start(bf16[128,256]{1,0:T(8,128)(2,1)S(1)} %get-tuple-element.78), channel_id=1, source_target_pairs={{4,0},{8,4},{12,8},{16,12},{20,16},{24,20},{28,24},{32,28},{36,32}... | collective-permute-start | bytes 196616 | tf_op jit(solution)/shard_map/ppermute | solution.py:23
  359.9 6.4 %copy-start.1 = (bf16[512,512]{1,0:T(8,128)(2,1)S(1)}, bf16[512,512]{1,0:T(8,128)(2,1)}, u32[]{:S(2)}) copy-start(bf16[512,512]{1,0:T(8,128)(2,1)} %param.8) | copy-start | bytes 1572868
Sparse Core Ops, SparseCore 0:
  32.0 88.4 all-gather.4
  123.2 91.6 all-gather.2
where the time goes:
time: 375 us; the launch traced here: 373 us
  waiting for transfers between devices  137 us (37%)
  local copies, waits for them, and re-layouts  72.6 us (19%)
  blocking collectives  54.3 us (14%)
  starting transfers between devices  36.7 us (10%)
  matrix products  31.9 us (9%)
  other arithmetic  22.1 us (6%)
  between operations  18.8 us (5%)
    all_gather x2, waiting for transfers between devices, picked(): lax.all_gather(shard, axis)  88.3 us
    all_to_all x1, blocking collectives, on_device(): lax.all_to_all(output_rows, 'head', split_axis=0, concat_axis=1, tiled=True)  54.3 us
    all_to_all x1, waiting for transfers between devices, on_device(): lax.all_to_all(query_rows, 'head', split_axis=1, concat_axis=0, tiled=True)  35.6 us
    all_to_all x3, local copies, waits for them, and re-layouts, on_device(): lax.all_to_all(output_rows, 'head', split_axis=0, concat_axis=1, tiled=True)  20 us
    dot_general x4, matrix products, attend_group(): jnp.einsum('pgts,psd->ptgd', rounded, values, preferred_element_type=jnp....  19.8 us
    all_to_all x1, starting transfers between devices, on_device(): lax.all_to_all(outgoing, 'seq', split_axis=0, concat_axis=0, tiled=True)  17.9 us
    reduce_sum x4, other arithmetic, attend_group(): row_total = jnp.sum(weights, axis=-1)  15 us
    dot_general x4, matrix products, attend_group(): jnp.einsum('ptgd,psd->pgts', query_group, key_part, preferred_element_typ...  12.1 us
  transfers between devices with their start and end apart: 8, of which 6 were waited for; matrix products, arithmetic and copies ran while one was open for 8% of the time, Pallas kernels for 0%

commit v1 on v0

--- a/solution.py
+++ b/solution.py
@@ -50,7 +50,12 @@
 
 def on_device(query_rows, key_rows, value_rows, random_table, global_blocks):
     queries, key_part, values = (
-        lax.all_to_all(query_rows, "head", split_axis=1, concat_axis=0, tiled=True),
+        jnp.concatenate(
+            lax.all_to_all(
+                jnp.stack(jnp.split(query_rows, lax.axis_size("head"), axis=1)), "head", 0, 0
+            ),
+            axis=0,
+        ),
         lax.all_to_all(key_rows, "head", split_axis=1, concat_axis=0, tiled=True),
         lax.all_to_all(value_rows, "head", split_axis=1, concat_axis=0, tiled=True),
     )

time: 375 us -> 375 us (level)
    all_to_all x1 -> x0, local copies, waits for them, and re-layouts: 4.72 us -> none  [on_device(): lax.all_to_all(query_rows, 'head', split_axis=1, concat_axis=0, tiled=True)]
where the time goes in v1:
time: 375 us; the launch traced here: 373 us
  waiting for transfers between devices  137 us (37%)
  local copies, waits for them, and re-layouts  70.5 us (19%)
  blocking collectives  54.3 us (14%)
  starting transfers between devices  36.6 us (10%)
  matrix products  31.9 us (9%)
  other arithmetic  24.3 us (6%)
  between operations  18.6 us (5%)
    all_gather x2, waiting for transfers between devices, picked(): lax.all_gather(shard, axis)  88.3 us
    all_to_all x1, blocking collectives, on_device(): lax.all_to_all(output_rows, 'head', split_axis=0, concat_axis=1, tiled=True)  54.3 us
    all_to_all x1, waiting for transfers between devices, on_device(): lax.all_to_all(jnp.stack(jnp.split(query_rows, lax.axis_size('head'), axi...  35.6 us
    all_to_all x3, local copies, waits for them, and re-layouts, on_device(): lax.all_to_all(output_rows, 'head', split_axis=0, concat_axis=1, tiled=True)  20 us
    dot_general x4, matrix products, attend_group(): jnp.einsum('pgts,psd->ptgd', rounded, values, preferred_element_type=jnp....  19.8 us
    all_to_all x1, starting transfers between devices, on_device(): lax.all_to_all(outgoing, 'seq', split_axis=0, concat_axis=0, tiled=True)  17.9 us
    reduce_sum x4, other arithmetic, attend_group(): row_total = jnp.sum(weights, axis=-1)  15 us
    dot_general x4, matrix products, attend_group(): jnp.einsum('ptgd,psd->pgts', query_group, key_part, preferred_element_typ...  12.1 us
  transfers between devices with their start and end apart: 8, of which 6 were waited for; matrix products, arithmetic and copies ran while one was open for 8% of the time, Pallas kernels for 0%

profile of v1, /device:TPU:1, one launch (start us, length us, event | category | flops | bytes accessed | tf_op | source)
XLA Modules:
  0.0 373.3 jit_solution(11673147134487753812)
XLA Ops:
  8.5 4.8 %all-to-all-start = ((bf16[512,4,128]{2,0,1:T(8,128)(2,1)}), bf16[512,4,128]{2,0,1:T(8,128)(2,1)S(1)}, u32[]{:S(2)}, u32[]{:S(2)}) async-start(bf16[512,4,128]{2,0,1:T(8,128)(2,1)} %copy_bitcast_fusion.3), calls=%async_computation | async-start | bytes 1048576 | tf_op jit(solution)/shard_map/all_to_all | solution.py:59
  13.3 1.9 copy_bitcast_fusion.2
  15.2 5.5 %all-to-all-done = bf16[512,4,128]{2,0,1:T(8,128)(2,1)S(1)} async-done(((bf16[512,4,128]{2,0,1:T(8,128)(2,1)}), bf16[512,4,128]{2,0,1:T(8,128)(2,1)S(1)}, u32[]{:S(2)}, u32[]{:S(2)}) %all-to-all-start) | async-done | bytes 524320 | tf_op jit(solution)/shard_map/all_to_all | solution.py:59
  20.8 3.5 all-to-all-start.1
  28.6 2.5 all-to-all-done.1
  31.8 2.6 slice_bitcast_fusion.7
  34.5 2.2 pad_maximum_fusion
  36.7 4.9 %all-to-all-start.3 = ((bf16[4,512,1024]{2,1,0:T(8,128)(2,1)}), bf16[4,512,1024]{2,1,0:T(8,128)(2,1)}, u32[]{:S(2)}, u32[]{:S(2)}) async-start(bf16[4,512,1024]{2,1,0:T(8,128)(2,1)} %pad_maximum_fusion), calls=%async_computation.3 | async-start | bytes 8388608 | tf_op jit(solution)/shard_map/all_to_all | solution.py:54
  44.0 2.8 gather_fusion
  46.8 4.0 %fusion.16 = bf16[64,1,128,256]{3,2,1,0:T(8,128)(2,1)} fusion(bf16[64,128,256]{2,1,0:T(8,128)(2,1)} %gather_fusion, pred[64]{0:T(512)(128)(4,1)S(1)} %compare_and_fusion, pred[64]{0:T(512)(128)(4,1)S(1)} %get-tuple-element.70), kind=kLoop, calls=%fused_computation.27 | loop fusion | flops 4194304 | bytes 8388736 | tf_op jit(solution)/shard_map/jit(_where)/select_n | solution.py:96
  50.8 35.6 %all-to-all-done.3 = bf16[4,512,1024]{2,1,0:T(8,128)(2,1)} async-done(((bf16[4,512,1024]{2,1,0:T(8,128)(2,1)}), bf16[4,512,1024]{2,1,0:T(8,128)(2,1)}, u32[]{:S(2)}, u32[]{:S(2)}) %all-to-all-start.3) | async-done | bytes 4194336 | tf_op jit(solution)/shard_map/all_to_all | solution.py:54
  86.4 17.9 %all-to-all-start.2 = ((bf16[64,1,128,256]{3,2,1,0:T(8,128)(2,1)}), bf16[64,1,128,256]{3,2,1,0:T(8,128)(2,1)}, u32[]{:S(2)}, u32[]{:S(2)}) async-start(bf16[64,1,128,256]{3,2,1,0:T(8,128)(2,1)} %fusion.16), calls=%async_computation.2 | async-start | bytes 8388608 | tf_op jit(solution)/shard_map/all_to_all | solution.py:97
  105.6 3.5 collective-permute-start
  109.2 1.9 collective-permute-start.1
  112.5 2.1 collective-permute-done
  114.6 2.8 collective-permute-done.1
  118.5 1.1 maximum_dynamic-update-slice_fusion
  119.6 1.1 constant_dynamic-update-slice_fusion.2
  120.7 5.2 %copy.76 = bf16[256,8,8,128]{3,2,1,0:T(8,128)(2,1)} copy(bf16[256,8,8,128]{3,1,2,0:T(8,128)(2,1)} %bitcast.54) | data formatting | bytes 8388608
  126.8 88.3 %all-gather.3.cloned.1.call-done = bf16[64,128,256]{2,1,0:T(8,128)(2,1)} async-done(((bf16[1,128,256]{2,1,0:T(8,128)(2,1)}), bf16[64,128,256]{2,1,0:T(8,128)(2,1)}) %all-gather.3.cloned.1.call-update) | async-done | bytes 4194320 | tf_op jit(solution)/shard_map/all_gather | solution.py:31
  215.9 1.5 broadcast_dynamic-update-slice_fusion
  217.5 4.7 %gather_fusion.2 = bf16[48,128,256]{2,1,0:T(8,128)(2,1)} fusion(bf16[64,1,128,256]{3,2,1,0:T(8,128)(2,1)} %all-to-all-done.2, s32[48]{0:T(128)S(1)} %fusion.35), kind=kCustom, calls=%fused_computation.2 | custom fusion | bytes 6291840 | tf_op jit(solution)/shard_map/gather | solution.py:105
  222.1 3.8 %constant_dynamic-update-slice_fusion.1 = bf16[4,4,1024,256]{3,2,1,0:T(8,128)(2,1)} fusion(bf16[4,4,1024,256]{3,2,1,0:T(8,128)(2,1)} %broadcast_dynamic-update-slice_fusion, bf16[4,4,384,256]{3,2,1,0:T(8,128)(2,1)} %bitcast.164), kind=kLoop, calls=%fused_computation.70 | loop fusion | bytes 6291456 | tf_op jit(solution)/shard_map/concatenate | solution.py:112
  226.0 66.2 %while.10 = (s32[]{:T(128)}, bf16[4,4,128,8,128]{4,3,2,1,0:T(8,128)(2,1)}, bf16[4,4,1024,256]{3,2,1,0:T(8,128)(2,1)}, pred[4,4,1024]{2,1,0:T(4,128)(4,1)S(1)}, bf16[4,4,128,8,128]{4,3,2,1,0:T(8,128)(2,1)}, /*index=5*/s32[]{:T(128)}) while((s32[]{:T(128)}, bf16[4,4,128,8,128]{4,3,2,1,0:T(8,128)(2,1)}, bf16[4,4,1024,256]{3,2,1,0:T(8,128)(2,1)}, ...), condition=%wide.region_9.10_spmd, body=%wide.region_6.9_spmd.sunk | while | flops 2194661376 | bytes 65114704 | solution.py:134
  226.0 1.7 dynamic-slice_bitcast_fusion.5
  227.7 1.3 constant_dynamic-slice_fusion.6
  229.0 3.0 bitcast_reduce_fusion.2
  232.1 3.7 %fusion.48 = f32[4,8,128]{2,1,0:T(8,128)S(1)} fusion(f32[4,1024,128,8]{2,1,3,0:T(8,128)S(1)} %get-tuple-element.121, f32[4,8,128]{2,1,0:T(8,128)S(1)} %get-tuple-element.122, pred[4,1024]{1,0:T(4,128)(4,1)S(1)} %dynamic-slice_bitcast_fusion.4), kind=kLoop, calls=%fused_computation.7.clone.1 | loop fusion | flops 16773120 | bytes 16814080 | tf_op jit(solution)/shard_map/while/body/eval_jaxpr/reduce_sum | solution.py:44
  235.8 5.0 %fusion.49 = bf16[1,4,128,8,128]{2,4,3,1,0:T(8,128)(2,1)S(1)} fusion(f32[4,1024,128,8]{2,1,3,0:T(8,128)S(1)} %get-tuple-element.121, f32[4,8,128]{2,1,0:T(8,128)S(1)} %get-tuple-element.122, pred[4,1024]{1,0:T(4,128)(4,1)S(1)} %dynamic-slice_bitcast_fusion.4, bf16[4,1024,256]{2,1,0:T(8,128)(2,1)S(1)} %dynamic-slice_bitcast_fusion.5, ...), kind=kOutput, calls=%fused_computation.14.clone.1 | convolution fusion | flops 1091567616 | bytes 18911232 | tf_op jit(solution)/shard_map/while/body/eval_jaxpr/pgts,psd->ptgd/dot_general | solution.py:46
  242.5 1.7 dynamic-slice_bitcast_fusion.5
  244.3 1.3 constant_dynamic-slice_fusion.6
  245.6 3.0 bitcast_reduce_fusion.2
  248.6 3.7 %fusion.48 = f32[4,8,128]{2,1,0:T(8,128)S(1)} fusion(f32[4,1024,128,8]{2,1,3,0:T(8,128)S(1)} %get-tuple-element.121, f32[4,8,128]{2,1,0:T(8,128)S(1)} %get-tuple-element.122, pred[4,1024]{1,0:T(4,128)(4,1)S(1)} %dynamic-slice_bitcast_fusion.4), kind=kLoop, calls=%fused_computation.7.clone.1 | loop fusion | flops 16773120 | bytes 16814080 | tf_op jit(solution)/shard_map/while/body/eval_jaxpr/reduce_sum | solution.py:44
  252.4 5.0 %fusion.49 = bf16[1,4,128,8,128]{2,4,3,1,0:T(8,128)(2,1)S(1)} fusion(f32[4,1024,128,8]{2,1,3,0:T(8,128)S(1)} %get-tuple-element.121, f32[4,8,128]{2,1,0:T(8,128)S(1)} %get-tuple-element.122, pred[4,1024]{1,0:T(4,128)(4,1)S(1)} %dynamic-slice_bitcast_fusion.4, bf16[4,1024,256]{2,1,0:T(8,128)(2,1)S(1)} %dynamic-slice_bitcast_fusion.5, ...), kind=kOutput, calls=%fused_computation.14.clone.1 | convolution fusion | flops 1091567616 | bytes 18911232 | tf_op jit(solution)/shard_map/while/body/eval_jaxpr/pgts,psd->ptgd/dot_general | solution.py:46
  259.1 1.7 dynamic-slice_bitcast_fusion.5
  260.8 1.3 constant_dynamic-slice_fusion.6
  262.1 3.0 bitcast_reduce_fusion.2
  265.2 3.7 %fusion.48 = f32[4,8,128]{2,1,0:T(8,128)S(1)} fusion(f32[4,1024,128,8]{2,1,3,0:T(8,128)S(1)} %get-tuple-element.121, f32[4,8,128]{2,1,0:T(8,128)S(1)} %get-tuple-element.122, pred[4,1024]{1,0:T(4,128)(4,1)S(1)} %dynamic-slice_bitcast_fusion.4), kind=kLoop, calls=%fused_computation.7.clone.1 | loop fusion | flops 16773120 | bytes 16814080 | tf_op jit(solution)/shard_map/while/body/eval_jaxpr/reduce_sum | solution.py:44
  268.9 5.0 %fusion.49 = bf16[1,4,128,8,128]{2,4,3,1,0:T(8,128)(2,1)S(1)} fusion(f32[4,1024,128,8]{2,1,3,0:T(8,128)S(1)} %get-tuple-element.121, f32[4,8,128]{2,1,0:T(8,128)S(1)} %get-tuple-element.122, pred[4,1024]{1,0:T(4,128)(4,1)S(1)} %dynamic-slice_bitcast_fusion.4, bf16[4,1024,256]{2,1,0:T(8,128)(2,1)S(1)} %dynamic-slice_bitcast_fusion.5, ...), kind=kOutput, calls=%fused_computation.14.clone.1 | convolution fusion | flops 1091567616 | bytes 18911232 | tf_op jit(solution)/shard_map/while/body/eval_jaxpr/pgts,psd->ptgd/dot_general | solution.py:46
  275.6 1.7 dynamic-slice_bitcast_fusion.5
  277.4 1.3 constant_dynamic-slice_fusion.6
  278.7 3.0 bitcast_reduce_fusion.2
  281.7 3.7 %fusion.48 = f32[4,8,128]{2,1,0:T(8,128)S(1)} fusion(f32[4,1024,128,8]{2,1,3,0:T(8,128)S(1)} %get-tuple-element.121, f32[4,8,128]{2,1,0:T(8,128)S(1)} %get-tuple-element.122, pred[4,1024]{1,0:T(4,128)(4,1)S(1)} %dynamic-slice_bitcast_fusion.4), kind=kLoop, calls=%fused_computation.7.clone.1 | loop fusion | flops 16773120 | bytes 16814080 | tf_op jit(solution)/shard_map/while/body/eval_jaxpr/reduce_sum | solution.py:44
  285.5 5.0 %fusion.49 = bf16[1,4,128,8,128]{2,4,3,1,0:T(8,128)(2,1)S(1)} fusion(f32[4,1024,128,8]{2,1,3,0:T(8,128)S(1)} %get-tuple-element.121, f32[4,8,128]{2,1,0:T(8,128)S(1)} %get-tuple-element.122, pred[4,1024]{1,0:T(4,128)(4,1)S(1)} %dynamic-slice_bitcast_fusion.4, bf16[4,1024,256]{2,1,0:T(8,128)(2,1)S(1)} %dynamic-slice_bitcast_fusion.5, ...), kind=kOutput, calls=%fused_computation.14.clone.1 | convolution fusion | flops 1091567616 | bytes 18911232 | tf_op jit(solution)/shard_map/while/body/eval_jaxpr/pgts,psd->ptgd/dot_general | solution.py:46
  292.2 7.3 %all_to_all.58 = bf16[4,512,1024]{2,1,0:T(8,128)(2,1)} reshape(bf16[4,4,128,8,128]{4,3,2,1,0:T(8,128)(2,1)} %get-tuple-element.32) | data formatting | bytes 8388608 | tf_op jit(solution)/shard_map/all_to_all | solution.py:136
  299.5 54.3 %all_to_all.67 = bf16[4,512,1024]{2,1,0:T(8,128)(2,1)} all-to-all(bf16[4,512,1024]{2,1,0:T(8,128)(2,1)} %all_to_all.58), channel_id=1, replica_groups=mesh['seq'=64,'head'=4] {'head'}, dimensions={0} | all-to-all | bytes 8388608 | tf_op jit(solution)/shard_map/all_to_all | solution.py:136
  353.8 6.3 %copy.64 = bf16[512,4,1024]{0,2,1:T(8,128)(2,1)} copy(bf16[512,4,1024]{2,0,1:T(8,128)(2,1)} %bitcast.162) | data formatting | bytes 8388608 | tf_op jit(solution)/shard_map/all_to_all | solution.py:136
  360.1 6.4 %copy.65 = bf16[512,4096]{1,0:T(8,128)(2,1)} copy(bf16[512,4096]{0,1:T(8,128)(2,1)} %bitcast.163) | data formatting | bytes 8388608 | tf_op jit(solution)/shard_map/all_to_all | solution.py:136
  (66 shorter events, 16.9 us)
Async XLA Ops:
  6.5 1.0 copy-start
  6.5 17.8 %copy-start.2 = (s32[2]{0:T(128)S(1)}, s32[2]{0:T(128)}, u32[]{:S(2)}) copy-start(s32[2]{0:T(128)} %param.11) | copy-start | bytes 28
  8.5 12.3 %all-to-all-start = ((bf16[512,4,128]{2,0,1:T(8,128)(2,1)}), bf16[512,4,128]{2,0,1:T(8,128)(2,1)S(1)}, u32[]{:S(2)}, u32[]{:S(2)}) async-start(bf16[512,4,128]{2,0,1:T(8,128)(2,1)} %copy_bitcast_fusion.3), calls=%async_computation | async-start | bytes 1048576 | tf_op jit(solution)/shard_map/all_to_all | solution.py:59
  20.8 10.4 %all-to-all-start.1 = ((bf16[512,4,128]{2,0,1:T(8,128)(2,1)}), bf16[512,4,128]{2,0,1:T(8,128)(2,1)S(1)}, u32[]{:S(2)}, u32[]{:S(2)}) async-start(bf16[512,4,128]{2,0,1:T(8,128)(2,1)} %copy_bitcast_fusion.2), calls=%async_computation.1 | async-start | bytes 1048576 | tf_op jit(solution)/shard_map/all_to_all | solution.py:60
  24.2 101.7 %all-gather.5.cloned.1.call-start = ((), (), s32[]{:S(2)}) async-start(), calls=%async_computation.6 | async-start | bytes 4259840 | tf_op jit(solution)/shard_map/all_gather | solution.py:31
  36.7 49.7 %all-to-all-start.3 = ((bf16[4,512,1024]{2,1,0:T(8,128)(2,1)}), bf16[4,512,1024]{2,1,0:T(8,128)(2,1)}, u32[]{:S(2)}, u32[]{:S(2)}) async-start(bf16[4,512,1024]{2,1,0:T(8,128)(2,1)} %pad_maximum_fusion), calls=%async_computation.3 | async-start | bytes 8388608 | tf_op jit(solution)/shard_map/all_to_all | solution.py:54
  41.6 173.5 %all-gather.3.cloned.1.call-start = ((), (), s32[]{:S(2)}) async-start(), calls=%async_computation.5 | async-start | bytes 4259840 | tf_op jit(solution)/shard_map/all_gather | solution.py:31
  86.4 131.1 %all-to-all-start.2 = ((bf16[64,1,128,256]{3,2,1,0:T(8,128)(2,1)}), bf16[64,1,128,256]{3,2,1,0:T(8,128)(2,1)}, u32[]{:S(2)}, u32[]{:S(2)}) async-start(bf16[64,1,128,256]{3,2,1,0:T(8,128)(2,1)} %fusion.16), calls=%async_computation.2 | async-start | bytes 8388608 | tf_op jit(solution)/shard_map/all_to_all | solution.py:97
  105.6 9.0 %collective-permute-start = (bf16[128,256]{1,0:T(8,128)(2,1)S(1)}, bf16[128,256]{1,0:T(8,128)(2,1)S(1)}, u32[]{:S(2)}, u32[]{:S(2)}) collective-permute-start(bf16[128,256]{1,0:T(8,128)(2,1)S(1)} %get-tuple-element.83), channel_id=1, source_target_pairs={{0,4},{4,8},{8,12},{12,16},{16,20},{20,24},{24,28},{28,32},{32,36}... | collective-permute-start | bytes 196616 | tf_op jit(solution)/shard_map/ppermute | solution.py:21
  109.2 8.2 %collective-permute-start.1 = (bf16[128,256]{1,0:T(8,128)(2,1)S(1)}, bf16[128,256]{1,0:T(8,128)(2,1)S(1)}, u32[]{:S(2)}, u32[]{:S(2)}) collective-permute-start(bf16[128,256]{1,0:T(8,128)(2,1)S(1)} %get-tuple-element.82), channel_id=1, source_target_pairs={{4,0},{8,4},{12,8},{16,12},{20,16},{24,20},{28,24},{32,28},{36,32}... | collective-permute-start | bytes 196616 | tf_op jit(solution)/shard_map/ppermute | solution.py:23
  360.1 6.4 %copy-start.1 = (bf16[512,512]{1,0:T(8,128)(2,1)S(1)}, bf16[512,512]{1,0:T(8,128)(2,1)}, u32[]{:S(2)}) copy-start(bf16[512,512]{1,0:T(8,128)(2,1)} %param.8) | copy-start | bytes 1572868
Sparse Core Ops, SparseCore 0:
  31.9 88.4 all-gather.4
  123.2 91.8 all-gather.2
